TPU v7x, 32 devices: a whole 2x2x4 slice. The times are simulated.
32 devices in a mesh: row: 4 (over y, x), col: 8 (over z, core).
Axes of the slice: x: 2, y: 2, z: 4, core: 2. Of those that a mesh axis runs over, the one named last changes fastest.
Arguments:
- depth: float32 [256, 4096], P('row', 'col'), may hold values from 0 to 1
- rainfall: float32 [256, 4096], P('row', 'col'), may hold values from 0.05 to 0.5
- conveyance: float32 [256, 4096], P('row', 'col'), may hold values from 0.2 to 5
- flow_dir: int32 [256, 4096], P('row', 'col'), may hold values from 0 to 7, as said below
- outlet: int32 [256, 4096], P('row', 'col'), may hold values 0 or 1
Outputs:
- new_depth: float32 [256, 4096], P('row', 'col')
- discharge: float32 [256, 4096], P('row', 'col')
Inputs may be any that keep to these rules, and one draw needn't show every extreme that they name: `flow_dir`: each cell's code is 0 to 7.
All inputs are finite; a program needn't handle non-finite values. No bound on the sum of `outlet` on one device may be relied on, other than what follows from the above.
Results may differ from a plain program's by a relative error of at most 0.00002.
Values sent between devices are 32-bit elements; how exact they have to be, the bound alone decides.
A program may use at most 64 MiB of HBM per device.

v0:
```python
import jax
import jax.numpy as jnp
from jax import lax
from jax.sharding import PartitionSpec as P

SUBSTEPS = 3
PASSES = 64


OFFSETS = ((0, 1), (1, 1), (1, 0), (1, -1), (0, -1), (-1, -1), (-1, 0), (-1, 1))


def extended(array, sides, width):
    for axis, dim in sides:
        peers, length = (lax.axis_size(axis), array.shape[dim])
        up = [(i, (i + 1) % peers) for i in range(peers - 1)]
        down = [(j, i) for i, j in up]
        last = lax.slice_in_dim(array, length - width, length, axis=dim)
        initial = lax.slice_in_dim(array, 0, width, axis=dim)
        before = lax.ppermute(last, axis, up)
        after = lax.ppermute(initial, axis, down)
        array = jnp.concatenate([before, array, after], axis=dim)
    return array


def padded_inflow(sent_pad, route_pad):
    rows = sent_pad.shape[0] - 2
    cols = sent_pad.shape[1] - 2
    total = jnp.zeros((rows, cols), jnp.float32)
    for k, (di, dj) in enumerate(OFFSETS):
        source = sent_pad[1 - di : 1 - di + rows, 1 - dj : 1 - dj + cols]
        target = route_pad[1 - di : 1 - di + rows, 1 - dj : 1 - dj + cols]
        total = total + jnp.where(target == k + 1, source, jnp.float32(0.0))
    return total


def on_device(depth, rainfall, conveyance, flow_dir, outlet):
    route = jnp.where(outlet == 1, 0, flow_dir + 1)
    length = jnp.where(flow_dir % 2 == 1, jnp.float32(0.70710678), jnp.float32(1.0))
    route_pad = extended(route, (("row", 0), ("col", 1)), 1)
    level = depth
    for step in range(SUBSTEPS):
        factor = conveyance * length * jnp.power(level, jnp.float32(2.0 / 3.0))
        share = factor / (1.0 + factor)
        out = level * share
        sent = jnp.where(route > 0, out, jnp.float32(0.0))
        sent_pad = extended(sent, (("row", 0), ("col", 1)), 1)
        level = level + rainfall - out + padded_inflow(sent_pad, route_pad)
    margin = 8
    route_wide = extended(route, (("row", 0), ("col", 1)), margin)
    level_wide = extended(level, (("row", 0), ("col", 1)), margin)
    rows, cols = level.shape

    def group_pass(index, acc):
        current = extended(acc, (("row", 0), ("col", 1)), margin)
        for inner in range(margin):
            edge = margin - inner
            route_here = route_wide[
                margin - edge : margin + rows + edge, margin - edge : margin + cols + edge
            ]
            level_here = level_wide[
                margin - edge + 1 : margin + rows + edge - 1,
                margin - edge + 1 : margin + cols + edge - 1,
            ]
            sent = jnp.where(route_here > 0, current, jnp.float32(0.0))
            current = level_here + padded_inflow(sent, route_here)
        return current

    acc = lax.fori_loop(0, PASSES // margin, group_pass, level)
    return (level, jnp.log(1.0 + acc))


def solution(mesh):
    placed = (P("row", "col"), P("row", "col"), P("row", "col"), P("row", "col"), P("row", "col"))
    return jax.shard_map(
        on_device,
        mesh=mesh,
        in_specs=placed,
        out_specs=(P("row", "col"), P("row", "col")),
        check_vma=False,
    )
```

profile of v0, /device:TPU:0, one launch (start us, length us, event | category | flops | bytes accessed | tf_op | source)
XLA Modules:
  0.0 261.8 jit_solution(14108373499394665814)
XLA Ops:
  0.6 1.4 broadcast_select_fusion.2
  2.0 4.9 %collective-permute-start.4 = (s32[1,512]{1,0:T(1,128)S(1)}, s32[1,512]{1,0:T(1,128)S(1)}, u32[]{:S(2)}, u32[]{:S(2)}) collective-permute-start(s32[1,512]{1,0:T(1,128)S(1)} %get-tuple-element.88), channel_id=1, source_target_pairs={{0,8},{8,16},{16,24},{1,9},{9,17},{17,25},{2,10},{10,18},{18,26},{... | collective-permute-start | bytes 6152 | tf_op jit(solution)/shard_map/ppermute | solution.py:20
  6.9 1.3 collective-permute-start.5
  8.2 4.5 %collective-permute-start.7 = (f32[1,512]{1,0:T(1,128)S(1)}, f32[1,512]{1,0:T(1,128)S(1)}, u32[]{:S(2)}, u32[]{:S(2)}) collective-permute-start(f32[1,512]{1,0:T(1,128)S(1)} %get-tuple-element.90), channel_id=1, source_target_pairs={{0,8},{8,16},{16,24},{1,9},{9,17},{17,25},{2,10},{10,18},{18,26},{... | collective-permute-start | bytes 6152 | tf_op jit(solution)/shard_map/ppermute | solution.py:20
  12.7 1.3 collective-permute-start.8
  15.4 3.0 %collective-permute-start.6 = (s32[66,1]{1,0:T(8,128)S(1)}, s32[66,1]{1,0:T(8,128)S(1)}, u32[]{:S(2)}, u32[]{:S(2)}) collective-permute-start(s32[66,1]{1,0:T(8,128)S(1)} %get-tuple-element.75), channel_id=1, source_target_pairs={{0,1},{1,2},{2,3},{3,4},{4,5},{5,6},{6,7},{8,9},{9,10},{10,11},{11... | collective-permute-start | bytes 800 | tf_op jit(solution)/shard_map/ppermute | solution.py:20
  20.0 3.6 %collective-permute-start.9 = (f32[66,1]{1,0:T(8,128)S(1)}, f32[66,1]{1,0:T(8,128)S(1)}, u32[]{:S(2)}, u32[]{:S(2)}) collective-permute-start(f32[66,1]{1,0:T(8,128)S(1)} %get-tuple-element.79), channel_id=1, source_target_pairs={{0,1},{1,2},{2,3},{3,4},{4,5},{5,6},{6,7},{8,9},{9,10},{10,11},{11... | collective-permute-start | bytes 800 | tf_op jit(solution)/shard_map/ppermute | solution.py:20
  25.5 4.9 %collective-permute-start.12 = (f32[1,512]{1,0:T(1,128)S(1)}, f32[1,512]{1,0:T(1,128)S(1)}, u32[]{:S(2)}, u32[]{:S(2)}) collective-permute-start(f32[1,512]{1,0:T(1,128)S(1)} %get-tuple-element.86), channel_id=1, source_target_pairs={{0,8},{8,16},{16,24},{1,9},{9,17},{17,25},{2,10},{10,18},{18,26},{... | collective-permute-start | bytes 6152 | tf_op jit(solution)/shard_map/ppermute | solution.py:20
  31.7 5.1 %collective-permute-done.13 = f32[1,512]{1,0:T(1,128)S(1)} collective-permute-done((f32[1,512]{1,0:T(1,128)S(1)}, f32[1,512]{1,0:T(1,128)S(1)}, u32[]{:S(2)}, u32[]{:S(2)}) %collective-permute-start.13) | collective-permute-done | bytes 2080 | tf_op jit(solution)/shard_map/ppermute | solution.py:21
  36.9 2.6 collective-permute-start.14
  40.8 4.8 %collective-permute-done.15 = f32[66,1]{1,0:T(8,128)S(1)} collective-permute-done((f32[66,1]{1,0:T(8,128)S(1)}, f32[66,1]{1,0:T(8,128)S(1)}, u32[]{:S(2)}, u32[]{:S(2)}) %collective-permute-start.15) | collective-permute-done | bytes 296 | tf_op jit(solution)/shard_map/ppermute | solution.py:21
  46.3 4.8 %collective-permute-start.16 = (f32[1,512]{1,0:T(1,128)S(1)}, f32[1,512]{1,0:T(1,128)S(1)}, u32[]{:S(2)}, u32[]{:S(2)}) collective-permute-start(f32[1,512]{1,0:T(1,128)S(1)} %get-tuple-element.84), channel_id=1, source_target_pairs={{0,8},{8,16},{16,24},{1,9},{9,17},{17,25},{2,10},{10,18},{18,26},{... | collective-permute-start | bytes 6152 | tf_op jit(solution)/shard_map/ppermute | solution.py:20
  52.4 4.5 %collective-permute-start.20 = (s32[8,512]{1,0:T(8,128)S(1)}, s32[8,512]{1,0:T(8,128)S(1)}, u32[]{:S(2)}, u32[]{:S(2)}) collective-permute-start(s32[8,512]{1,0:T(8,128)S(1)} %get-tuple-element.82), channel_id=1, source_target_pairs={{0,8},{8,16},{16,24},{1,9},{9,17},{17,25},{2,10},{10,18},{18,26},{... | collective-permute-start | bytes 49160 | tf_op jit(solution)/shard_map/ppermute | solution.py:20
  57.1 3.7 %collective-permute-start.18 = (f32[66,1]{1,0:T(8,128)S(1)}, f32[66,1]{1,0:T(8,128)S(1)}, u32[]{:S(2)}, u32[]{:S(2)}) collective-permute-start(f32[66,1]{1,0:T(8,128)S(1)} %get-tuple-element.67), channel_id=1, source_target_pairs={{0,1},{1,2},{2,3},{3,4},{4,5},{5,6},{6,7},{8,9},{9,10},{10,11},{11... | collective-permute-start | bytes 800 | tf_op jit(solution)/shard_map/ppermute | solution.py:20
  64.8 3.7 %collective-permute-start.24 = (f32[8,512]{1,0:T(8,128)S(1)}, f32[8,512]{1,0:T(8,128)S(1)}, u32[]{:S(2)}, u32[]{:S(2)}) collective-permute-start(f32[8,512]{1,0:T(8,128)S(1)} %get-tuple-element.80), channel_id=1, source_target_pairs={{0,8},{8,16},{16,24},{1,9},{9,17},{17,25},{2,10},{10,18},{18,26},{... | collective-permute-start | bytes 49160 | tf_op jit(solution)/shard_map/ppermute | solution.py:20
  68.5 1.3 collective-permute-start.25
  69.9 3.4 %collective-permute-start.22 = (s32[80,8]{1,0:T(8,128)S(1)}, s32[80,8]{1,0:T(8,128)S(1)}, u32[]{:S(2)}, u32[]{:S(2)}) collective-permute-start(s32[80,8]{1,0:T(8,128)S(1)} %get-tuple-element.62), channel_id=1, source_target_pairs={{0,1},{1,2},{2,3},{3,4},{4,5},{5,6},{6,7},{8,9},{9,10},{10,11},{11... | collective-permute-start | bytes 7688 | tf_op jit(solution)/shard_map/ppermute | solution.py:20
  74.7 4.2 %collective-permute-start.26 = (f32[80,8]{1,0:T(8,128)S(1)}, f32[80,8]{1,0:T(8,128)S(1)}, u32[]{:S(2)}, u32[]{:S(2)}) collective-permute-start(f32[80,8]{1,0:T(8,128)S(1)} %get-tuple-element.60), channel_id=1, source_target_pairs={{0,1},{1,2},{2,3},{3,4},{4,5},{5,6},{6,7},{8,9},{9,10},{10,11},{11... | collective-permute-start | bytes 7688 | tf_op jit(solution)/shard_map/ppermute | solution.py:20
  79.0 1.3 collective-permute-start.27
  80.5 2.9 %collective-permute-done.27 = f32[80,8]{1,0:T(8,128)S(1)} collective-permute-done((f32[80,8]{1,0:T(8,128)S(1)}, f32[80,8]{1,0:T(8,128)S(1)}, u32[]{:S(2)}, u32[]{:S(2)}) %collective-permute-start.27) | collective-permute-done | bytes 2592 | tf_op jit(solution)/shard_map/ppermute | solution.py:21
  83.5 177.6 %while.10 = (s32[]{:T(128)}, f32[64,512]{1,0:T(8,128)S(1)}, s32[80,528]{1,0:T(8,128)S(1)}, f32[80,528]{1,0:T(8,128)S(1)}, f32[64,512]{1,0:T(8,128)S(1)}, /*index=5*/s32[]{:T(128)}) while((s32[]{:T(128)}, f32[64,512]{1,0:T(8,128)S(1)}, s32[80,528]{1,0:T(8,128)S(1)}, f32[80,528]{1,0:T(8,128)S(1)}, f32[64,512]{1,0:T(8,128)S(1)}, ...), condition=%wide.region_1.2_spmd, body=%wide.region_0.1_spmd.sunk | while | flops 7772386 | bytes 23348004 | solution.py:69
  83.5 4.5 %collective-permute-start = (f32[8,512]{1,0:T(8,128)S(1)}, f32[8,512]{1,0:T(8,128)S(1)}, u32[]{:S(2)}, u32[]{:S(2)}) collective-permute-start(f32[8,512]{1,0:T(8,128)S(1)} %get-tuple-element.127), channel_id=1, source_target_pairs={{0,8},{8,16},{16,24},{1,9},{9,17},{17,25},{2,10},{10,18},{18,26},{... | collective-permute-start | bytes 49160 | tf_op jit(solution)/shard_map/while/body/eval_jaxpr/ppermute | solution.py:20
  88.1 1.3 collective-permute-start.1
  89.5 4.9 %collective-permute-done.1 = f32[8,512]{1,0:T(8,128)S(1)} collective-permute-done((f32[8,512]{1,0:T(8,128)S(1)}, f32[8,512]{1,0:T(8,128)S(1)}, u32[]{:S(2)}, u32[]{:S(2)}) %collective-permute-start.1) | collective-permute-done | bytes 16416 | tf_op jit(solution)/shard_map/while/body/eval_jaxpr/ppermute | solution.py:21
  95.8 4.1 %collective-permute-start.3 = (f32[80,8]{1,0:T(8,128)S(1)}, f32[80,8]{1,0:T(8,128)S(1)}, u32[]{:S(2)}, u32[]{:S(2)}) collective-permute-start(f32[80,8]{1,0:T(8,128)S(1)} %get-tuple-element.130), channel_id=1, source_target_pairs={{0,1},{1,2},{2,3},{3,4},{4,5},{5,6},{6,7},{8,9},{9,10},{10,11},{11... | collective-permute-start | bytes 7688 | tf_op jit(solution)/shard_map/while/body/eval_jaxpr/ppermute | solution.py:20
  107.0 4.5 %collective-permute-start = (f32[8,512]{1,0:T(8,128)S(1)}, f32[8,512]{1,0:T(8,128)S(1)}, u32[]{:S(2)}, u32[]{:S(2)}) collective-permute-start(f32[8,512]{1,0:T(8,128)S(1)} %get-tuple-element.127), channel_id=1, source_target_pairs={{0,8},{8,16},{16,24},{1,9},{9,17},{17,25},{2,10},{10,18},{18,26},{... | collective-permute-start | bytes 49160 | tf_op jit(solution)/shard_map/while/body/eval_jaxpr/ppermute | solution.py:20
  113.0 4.2 %collective-permute-done.1 = f32[8,512]{1,0:T(8,128)S(1)} collective-permute-done((f32[8,512]{1,0:T(8,128)S(1)}, f32[8,512]{1,0:T(8,128)S(1)}, u32[]{:S(2)}, u32[]{:S(2)}) %collective-permute-start.1) | collective-permute-done | bytes 16416 | tf_op jit(solution)/shard_map/while/body/eval_jaxpr/ppermute | solution.py:21
  118.5 3.1 %collective-permute-start.3 = (f32[80,8]{1,0:T(8,128)S(1)}, f32[80,8]{1,0:T(8,128)S(1)}, u32[]{:S(2)}, u32[]{:S(2)}) collective-permute-start(f32[80,8]{1,0:T(8,128)S(1)} %get-tuple-element.130), channel_id=1, source_target_pairs={{0,1},{1,2},{2,3},{3,4},{4,5},{5,6},{6,7},{8,9},{9,10},{10,11},{11... | collective-permute-start | bytes 7688 | tf_op jit(solution)/shard_map/while/body/eval_jaxpr/ppermute | solution.py:20
  128.7 3.1 %collective-permute-start = (f32[8,512]{1,0:T(8,128)S(1)}, f32[8,512]{1,0:T(8,128)S(1)}, u32[]{:S(2)}, u32[]{:S(2)}) collective-permute-start(f32[8,512]{1,0:T(8,128)S(1)} %get-tuple-element.127), channel_id=1, source_target_pairs={{0,8},{8,16},{16,24},{1,9},{9,17},{17,25},{2,10},{10,18},{18,26},{... | collective-permute-start | bytes 49160 | tf_op jit(solution)/shard_map/while/body/eval_jaxpr/ppermute | solution.py:20
  131.9 1.3 collective-permute-start.1
  133.3 4.2 %collective-permute-done.1 = f32[8,512]{1,0:T(8,128)S(1)} collective-permute-done((f32[8,512]{1,0:T(8,128)S(1)}, f32[8,512]{1,0:T(8,128)S(1)}, u32[]{:S(2)}, u32[]{:S(2)}) %collective-permute-start.1) | collective-permute-done | bytes 16416 | tf_op jit(solution)/shard_map/while/body/eval_jaxpr/ppermute | solution.py:21
  138.9 4.8 %collective-permute-start.3 = (f32[80,8]{1,0:T(8,128)S(1)}, f32[80,8]{1,0:T(8,128)S(1)}, u32[]{:S(2)}, u32[]{:S(2)}) collective-permute-start(f32[80,8]{1,0:T(8,128)S(1)} %get-tuple-element.130), channel_id=1, source_target_pairs={{0,1},{1,2},{2,3},{3,4},{4,5},{5,6},{6,7},{8,9},{9,10},{10,11},{11... | collective-permute-start | bytes 7688 | tf_op jit(solution)/shard_map/while/body/eval_jaxpr/ppermute | solution.py:20
  150.8 3.1 %collective-permute-start = (f32[8,512]{1,0:T(8,128)S(1)}, f32[8,512]{1,0:T(8,128)S(1)}, u32[]{:S(2)}, u32[]{:S(2)}) collective-permute-start(f32[8,512]{1,0:T(8,128)S(1)} %get-tuple-element.127), channel_id=1, source_target_pairs={{0,8},{8,16},{16,24},{1,9},{9,17},{17,25},{2,10},{10,18},{18,26},{... | collective-permute-start | bytes 49160 | tf_op jit(solution)/shard_map/while/body/eval_jaxpr/ppermute | solution.py:20
  155.4 4.2 %collective-permute-done.1 = f32[8,512]{1,0:T(8,128)S(1)} collective-permute-done((f32[8,512]{1,0:T(8,128)S(1)}, f32[8,512]{1,0:T(8,128)S(1)}, u32[]{:S(2)}, u32[]{:S(2)}) %collective-permute-start.1) | collective-permute-done | bytes 16416 | tf_op jit(solution)/shard_map/while/body/eval_jaxpr/ppermute | solution.py:21
  160.9 4.8 %collective-permute-start.3 = (f32[80,8]{1,0:T(8,128)S(1)}, f32[80,8]{1,0:T(8,128)S(1)}, u32[]{:S(2)}, u32[]{:S(2)}) collective-permute-start(f32[80,8]{1,0:T(8,128)S(1)} %get-tuple-element.130), channel_id=1, source_target_pairs={{0,1},{1,2},{2,3},{3,4},{4,5},{5,6},{6,7},{8,9},{9,10},{10,11},{11... | collective-permute-start | bytes 7688 | tf_op jit(solution)/shard_map/while/body/eval_jaxpr/ppermute | solution.py:20
  172.9 3.1 %collective-permute-start = (f32[8,512]{1,0:T(8,128)S(1)}, f32[8,512]{1,0:T(8,128)S(1)}, u32[]{:S(2)}, u32[]{:S(2)}) collective-permute-start(f32[8,512]{1,0:T(8,128)S(1)} %get-tuple-element.127), channel_id=1, source_target_pairs={{0,8},{8,16},{16,24},{1,9},{9,17},{17,25},{2,10},{10,18},{18,26},{... | collective-permute-start | bytes 49160 | tf_op jit(solution)/shard_map/while/body/eval_jaxpr/ppermute | solution.py:20
  177.4 4.2 %collective-permute-done.1 = f32[8,512]{1,0:T(8,128)S(1)} collective-permute-done((f32[8,512]{1,0:T(8,128)S(1)}, f32[8,512]{1,0:T(8,128)S(1)}, u32[]{:S(2)}, u32[]{:S(2)}) %collective-permute-start.1) | collective-permute-done | bytes 16416 | tf_op jit(solution)/shard_map/while/body/eval_jaxpr/ppermute | solution.py:21
  183.0 4.8 %collective-permute-start.3 = (f32[80,8]{1,0:T(8,128)S(1)}, f32[80,8]{1,0:T(8,128)S(1)}, u32[]{:S(2)}, u32[]{:S(2)}) collective-permute-start(f32[80,8]{1,0:T(8,128)S(1)} %get-tuple-element.130), channel_id=1, source_target_pairs={{0,1},{1,2},{2,3},{3,4},{4,5},{5,6},{6,7},{8,9},{9,10},{10,11},{11... | collective-permute-start | bytes 7688 | tf_op jit(solution)/shard_map/while/body/eval_jaxpr/ppermute | solution.py:20
  194.9 3.1 %collective-permute-start = (f32[8,512]{1,0:T(8,128)S(1)}, f32[8,512]{1,0:T(8,128)S(1)}, u32[]{:S(2)}, u32[]{:S(2)}) collective-permute-start(f32[8,512]{1,0:T(8,128)S(1)} %get-tuple-element.127), channel_id=1, source_target_pairs={{0,8},{8,16},{16,24},{1,9},{9,17},{17,25},{2,10},{10,18},{18,26},{... | collective-permute-start | bytes 49160 | tf_op jit(solution)/shard_map/while/body/eval_jaxpr/ppermute | solution.py:20
  198.0 1.3 collective-permute-start.1
  199.5 4.2 %collective-permute-done.1 = f32[8,512]{1,0:T(8,128)S(1)} collective-permute-done((f32[8,512]{1,0:T(8,128)S(1)}, f32[8,512]{1,0:T(8,128)S(1)}, u32[]{:S(2)}, u32[]{:S(2)}) %collective-permute-start.1) | collective-permute-done | bytes 16416 | tf_op jit(solution)/shard_map/while/body/eval_jaxpr/ppermute | solution.py:21
  205.0 4.8 %collective-permute-start.3 = (f32[80,8]{1,0:T(8,128)S(1)}, f32[80,8]{1,0:T(8,128)S(1)}, u32[]{:S(2)}, u32[]{:S(2)}) collective-permute-start(f32[80,8]{1,0:T(8,128)S(1)} %get-tuple-element.130), channel_id=1, source_target_pairs={{0,1},{1,2},{2,3},{3,4},{4,5},{5,6},{6,7},{8,9},{9,10},{10,11},{11... | collective-permute-start | bytes 7688 | tf_op jit(solution)/shard_map/while/body/eval_jaxpr/ppermute | solution.py:20
  217.0 3.1 %collective-permute-start = (f32[8,512]{1,0:T(8,128)S(1)}, f32[8,512]{1,0:T(8,128)S(1)}, u32[]{:S(2)}, u32[]{:S(2)}) collective-permute-start(f32[8,512]{1,0:T(8,128)S(1)} %get-tuple-element.127), channel_id=1, source_target_pairs={{0,8},{8,16},{16,24},{1,9},{9,17},{17,25},{2,10},{10,18},{18,26},{... | collective-permute-start | bytes 49160 | tf_op jit(solution)/shard_map/while/body/eval_jaxpr/ppermute | solution.py:20
  221.5 4.2 %collective-permute-done.1 = f32[8,512]{1,0:T(8,128)S(1)} collective-permute-done((f32[8,512]{1,0:T(8,128)S(1)}, f32[8,512]{1,0:T(8,128)S(1)}, u32[]{:S(2)}, u32[]{:S(2)}) %collective-permute-start.1) | collective-permute-done | bytes 16416 | tf_op jit(solution)/shard_map/while/body/eval_jaxpr/ppermute | solution.py:21
  227.1 4.8 %collective-permute-start.3 = (f32[80,8]{1,0:T(8,128)S(1)}, f32[80,8]{1,0:T(8,128)S(1)}, u32[]{:S(2)}, u32[]{:S(2)}) collective-permute-start(f32[80,8]{1,0:T(8,128)S(1)} %get-tuple-element.130), channel_id=1, source_target_pairs={{0,1},{1,2},{2,3},{3,4},{4,5},{5,6},{6,7},{8,9},{9,10},{10,11},{11... | collective-permute-start | bytes 7688 | tf_op jit(solution)/shard_map/while/body/eval_jaxpr/ppermute | solution.py:20
  239.0 3.1 %collective-permute-start = (f32[8,512]{1,0:T(8,128)S(1)}, f32[8,512]{1,0:T(8,128)S(1)}, u32[]{:S(2)}, u32[]{:S(2)}) collective-permute-start(f32[8,512]{1,0:T(8,128)S(1)} %get-tuple-element.127), channel_id=1, source_target_pairs={{0,8},{8,16},{16,24},{1,9},{9,17},{17,25},{2,10},{10,18},{18,26},{... | collective-permute-start | bytes 49160 | tf_op jit(solution)/shard_map/while/body/eval_jaxpr/ppermute | solution.py:20
  243.6 4.2 %collective-permute-done.1 = f32[8,512]{1,0:T(8,128)S(1)} collective-permute-done((f32[8,512]{1,0:T(8,128)S(1)}, f32[8,512]{1,0:T(8,128)S(1)}, u32[]{:S(2)}, u32[]{:S(2)}) %collective-permute-start.1) | collective-permute-done | bytes 16416 | tf_op jit(solution)/shard_map/while/body/eval_jaxpr/ppermute | solution.py:21
  249.2 4.8 %collective-permute-start.3 = (f32[80,8]{1,0:T(8,128)S(1)}, f32[80,8]{1,0:T(8,128)S(1)}, u32[]{:S(2)}, u32[]{:S(2)}) collective-permute-start(f32[80,8]{1,0:T(8,128)S(1)} %get-tuple-element.130), channel_id=1, source_target_pairs={{0,1},{1,2},{2,3},{3,4},{4,5},{5,6},{6,7},{8,9},{9,10},{10,11},{11... | collective-permute-start | bytes 7688 | tf_op jit(solution)/shard_map/while/body/eval_jaxpr/ppermute | solution.py:20
  (207 shorter events, 90.5 us)
Async XLA Ops:
  2.0 12.0 %collective-permute-start.4 = (s32[1,512]{1,0:T(1,128)S(1)}, s32[1,512]{1,0:T(1,128)S(1)}, u32[]{:S(2)}, u32[]{:S(2)}) collective-permute-start(s32[1,512]{1,0:T(1,128)S(1)} %get-tuple-element.88), channel_id=1, source_target_pairs={{0,8},{8,16},{16,24},{1,9},{9,17},{17,25},{2,10},{10,18},{18,26},{... | collective-permute-start | bytes 6152 | tf_op jit(solution)/shard_map/ppermute | solution.py:20
  6.9 7.2 %collective-permute-start.5 = (s32[1,512]{1,0:T(1,128)S(1)}, s32[1,512]{1,0:T(1,128)S(1)}, u32[]{:S(2)}, u32[]{:S(2)}) collective-permute-start(s32[1,512]{1,0:T(1,128)S(1)} %get-tuple-element.89), channel_id=1, source_target_pairs={{8,0},{16,8},{24,16},{9,1},{17,9},{25,17},{10,2},{18,10},{26,18},{... | collective-permute-start | bytes 6152 | tf_op jit(solution)/shard_map/ppermute | solution.py:21
  8.2 10.3 %collective-permute-start.7 = (f32[1,512]{1,0:T(1,128)S(1)}, f32[1,512]{1,0:T(1,128)S(1)}, u32[]{:S(2)}, u32[]{:S(2)}) collective-permute-start(f32[1,512]{1,0:T(1,128)S(1)} %get-tuple-element.90), channel_id=1, source_target_pairs={{0,8},{8,16},{16,24},{1,9},{9,17},{17,25},{2,10},{10,18},{18,26},{... | collective-permute-start | bytes 6152 | tf_op jit(solution)/shard_map/ppermute | solution.py:20
  12.7 5.9 %collective-permute-start.8 = (f32[1,512]{1,0:T(1,128)S(1)}, f32[1,512]{1,0:T(1,128)S(1)}, u32[]{:S(2)}, u32[]{:S(2)}) collective-permute-start(f32[1,512]{1,0:T(1,128)S(1)} %get-tuple-element.91), channel_id=1, source_target_pairs={{8,0},{16,8},{24,16},{9,1},{17,9},{25,17},{10,2},{18,10},{26,18},{... | collective-permute-start | bytes 6152 | tf_op jit(solution)/shard_map/ppermute | solution.py:21
  14.2 9.5 %collective-permute-start.10 = (s32[66,1]{1,0:T(8,128)S(1)}, s32[66,1]{1,0:T(8,128)S(1)}, u32[]{:S(2)}, u32[]{:S(2)}) collective-permute-start(s32[66,1]{1,0:T(8,128)S(1)} %get-tuple-element.74), channel_id=1, source_target_pairs={{1,0},{2,1},{3,2},{4,3},{5,4},{6,5},{7,6},{9,8},{10,9},{11,10},{12... | collective-permute-start | bytes 800 | tf_op jit(solution)/shard_map/ppermute | solution.py:21
  15.4 8.2 %collective-permute-start.6 = (s32[66,1]{1,0:T(8,128)S(1)}, s32[66,1]{1,0:T(8,128)S(1)}, u32[]{:S(2)}, u32[]{:S(2)}) collective-permute-start(s32[66,1]{1,0:T(8,128)S(1)} %get-tuple-element.75), channel_id=1, source_target_pairs={{0,1},{1,2},{2,3},{3,4},{4,5},{5,6},{6,7},{8,9},{9,10},{10,11},{11... | collective-permute-start | bytes 800 | tf_op jit(solution)/shard_map/ppermute | solution.py:20
  18.7 5.1 %collective-permute-start.11 = (f32[66,1]{1,0:T(8,128)S(1)}, f32[66,1]{1,0:T(8,128)S(1)}, u32[]{:S(2)}, u32[]{:S(2)}) collective-permute-start(f32[66,1]{1,0:T(8,128)S(1)} %get-tuple-element.78), channel_id=1, source_target_pairs={{1,0},{2,1},{3,2},{4,3},{5,4},{6,5},{7,6},{9,8},{10,9},{11,10},{12... | collective-permute-start | bytes 800 | tf_op jit(solution)/shard_map/ppermute | solution.py:21
  25.5 6.2 %collective-permute-start.12 = (f32[1,512]{1,0:T(1,128)S(1)}, f32[1,512]{1,0:T(1,128)S(1)}, u32[]{:S(2)}, u32[]{:S(2)}) collective-permute-start(f32[1,512]{1,0:T(1,128)S(1)} %get-tuple-element.86), channel_id=1, source_target_pairs={{0,8},{8,16},{16,24},{1,9},{9,17},{17,25},{2,10},{10,18},{18,26},{... | collective-permute-start | bytes 6152 | tf_op jit(solution)/shard_map/ppermute | solution.py:20
  30.4 6.4 %collective-permute-start.13 = (f32[1,512]{1,0:T(1,128)S(1)}, f32[1,512]{1,0:T(1,128)S(1)}, u32[]{:S(2)}, u32[]{:S(2)}) collective-permute-start(f32[1,512]{1,0:T(1,128)S(1)} %get-tuple-element.87), channel_id=1, source_target_pairs={{8,0},{16,8},{24,16},{9,1},{17,9},{25,17},{10,2},{18,10},{26,18},{... | collective-permute-start | bytes 6152 | tf_op jit(solution)/shard_map/ppermute | solution.py:21
  39.5 6.1 %collective-permute-start.15 = (f32[66,1]{1,0:T(8,128)S(1)}, f32[66,1]{1,0:T(8,128)S(1)}, u32[]{:S(2)}, u32[]{:S(2)}) collective-permute-start(f32[66,1]{1,0:T(8,128)S(1)} %get-tuple-element.70), channel_id=1, source_target_pairs={{1,0},{2,1},{3,2},{4,3},{5,4},{6,5},{7,6},{9,8},{10,9},{11,10},{12... | collective-permute-start | bytes 800 | tf_op jit(solution)/shard_map/ppermute | solution.py:21
  46.3 10.7 %collective-permute-start.16 = (f32[1,512]{1,0:T(1,128)S(1)}, f32[1,512]{1,0:T(1,128)S(1)}, u32[]{:S(2)}, u32[]{:S(2)}) collective-permute-start(f32[1,512]{1,0:T(1,128)S(1)} %get-tuple-element.84), channel_id=1, source_target_pairs={{0,8},{8,16},{16,24},{1,9},{9,17},{17,25},{2,10},{10,18},{18,26},{... | collective-permute-start | bytes 6152 | tf_op jit(solution)/shard_map/ppermute | solution.py:20
  51.1 5.9 %collective-permute-start.17 = (f32[1,512]{1,0:T(1,128)S(1)}, f32[1,512]{1,0:T(1,128)S(1)}, u32[]{:S(2)}, u32[]{:S(2)}) collective-permute-start(f32[1,512]{1,0:T(1,128)S(1)} %get-tuple-element.85), channel_id=1, source_target_pairs={{8,0},{16,8},{24,16},{9,1},{17,9},{25,17},{10,2},{18,10},{26,18},{... | collective-permute-start | bytes 6152 | tf_op jit(solution)/shard_map/ppermute | solution.py:21
  52.4 17.4 %collective-permute-start.20 = (s32[8,512]{1,0:T(8,128)S(1)}, s32[8,512]{1,0:T(8,128)S(1)}, u32[]{:S(2)}, u32[]{:S(2)}) collective-permute-start(s32[8,512]{1,0:T(8,128)S(1)} %get-tuple-element.82), channel_id=1, source_target_pairs={{0,8},{8,16},{16,24},{1,9},{9,17},{17,25},{2,10},{10,18},{18,26},{... | collective-permute-start | bytes 49160 | tf_op jit(solution)/shard_map/ppermute | solution.py:20
  57.1 6.3 %collective-permute-start.18 = (f32[66,1]{1,0:T(8,128)S(1)}, f32[66,1]{1,0:T(8,128)S(1)}, u32[]{:S(2)}, u32[]{:S(2)}) collective-permute-start(f32[66,1]{1,0:T(8,128)S(1)} %get-tuple-element.67), channel_id=1, source_target_pairs={{0,1},{1,2},{2,3},{3,4},{4,5},{5,6},{6,7},{8,9},{9,10},{10,11},{11... | collective-permute-start | bytes 800 | tf_op jit(solution)/shard_map/ppermute | solution.py:20
  62.1 7.8 %collective-permute-start.21 = (s32[8,512]{1,0:T(8,128)S(1)}, s32[8,512]{1,0:T(8,128)S(1)}, u32[]{:S(2)}, u32[]{:S(2)}) collective-permute-start(s32[8,512]{1,0:T(8,128)S(1)} %get-tuple-element.83), channel_id=1, source_target_pairs={{8,0},{16,8},{24,16},{9,1},{17,9},{25,17},{10,2},{18,10},{26,18},{... | collective-permute-start | bytes 49160 | tf_op jit(solution)/shard_map/ppermute | solution.py:21
  64.8 9.8 %collective-permute-start.24 = (f32[8,512]{1,0:T(8,128)S(1)}, f32[8,512]{1,0:T(8,128)S(1)}, u32[]{:S(2)}, u32[]{:S(2)}) collective-permute-start(f32[8,512]{1,0:T(8,128)S(1)} %get-tuple-element.80), channel_id=1, source_target_pairs={{0,8},{8,16},{16,24},{1,9},{9,17},{17,25},{2,10},{10,18},{18,26},{... | collective-permute-start | bytes 49160 | tf_op jit(solution)/shard_map/ppermute | solution.py:20
  68.5 6.1 %collective-permute-start.25 = (f32[8,512]{1,0:T(8,128)S(1)}, f32[8,512]{1,0:T(8,128)S(1)}, u32[]{:S(2)}, u32[]{:S(2)}) collective-permute-start(f32[8,512]{1,0:T(8,128)S(1)} %get-tuple-element.81), channel_id=1, source_target_pairs={{8,0},{16,8},{24,16},{9,1},{17,9},{25,17},{10,2},{18,10},{26,18},{... | collective-permute-start | bytes 49160 | tf_op jit(solution)/shard_map/ppermute | solution.py:21
  69.9 10.3 %collective-permute-start.22 = (s32[80,8]{1,0:T(8,128)S(1)}, s32[80,8]{1,0:T(8,128)S(1)}, u32[]{:S(2)}, u32[]{:S(2)}) collective-permute-start(s32[80,8]{1,0:T(8,128)S(1)} %get-tuple-element.62), channel_id=1, source_target_pairs={{0,1},{1,2},{2,3},{3,4},{4,5},{5,6},{6,7},{8,9},{9,10},{10,11},{11... | collective-permute-start | bytes 7688 | tf_op jit(solution)/shard_map/ppermute | solution.py:20
  73.3 7.0 %collective-permute-start.23 = (s32[80,8]{1,0:T(8,128)S(1)}, s32[80,8]{1,0:T(8,128)S(1)}, u32[]{:S(2)}, u32[]{:S(2)}) collective-permute-start(s32[80,8]{1,0:T(8,128)S(1)} %get-tuple-element.63), channel_id=1, source_target_pairs={{1,0},{2,1},{3,2},{4,3},{5,4},{6,5},{7,6},{9,8},{10,9},{11,10},{12... | collective-permute-start | bytes 7688 | tf_op jit(solution)/shard_map/ppermute | solution.py:21
  74.7 5.7 %collective-permute-start.26 = (f32[80,8]{1,0:T(8,128)S(1)}, f32[80,8]{1,0:T(8,128)S(1)}, u32[]{:S(2)}, u32[]{:S(2)}) collective-permute-start(f32[80,8]{1,0:T(8,128)S(1)} %get-tuple-element.60), channel_id=1, source_target_pairs={{0,1},{1,2},{2,3},{3,4},{4,5},{5,6},{6,7},{8,9},{9,10},{10,11},{11... | collective-permute-start | bytes 7688 | tf_op jit(solution)/shard_map/ppermute | solution.py:20
  83.5 6.0 %collective-permute-start = (f32[8,512]{1,0:T(8,128)S(1)}, f32[8,512]{1,0:T(8,128)S(1)}, u32[]{:S(2)}, u32[]{:S(2)}) collective-permute-start(f32[8,512]{1,0:T(8,128)S(1)} %get-tuple-element.127), channel_id=1, source_target_pairs={{0,8},{8,16},{16,24},{1,9},{9,17},{17,25},{2,10},{10,18},{18,26},{... | collective-permute-start | bytes 49160 | tf_op jit(solution)/shard_map/while/body/eval_jaxpr/ppermute | solution.py:20
  88.1 6.3 %collective-permute-start.1 = (f32[8,512]{1,0:T(8,128)S(1)}, f32[8,512]{1,0:T(8,128)S(1)}, u32[]{:S(2)}, u32[]{:S(2)}) collective-permute-start(f32[8,512]{1,0:T(8,128)S(1)} %get-tuple-element.128), channel_id=1, source_target_pairs={{8,0},{16,8},{24,16},{9,1},{17,9},{25,17},{10,2},{18,10},{26,18},{... | collective-permute-start | bytes 49160 | tf_op jit(solution)/shard_map/while/body/eval_jaxpr/ppermute | solution.py:21
  94.5 5.4 %collective-permute-start.2 = (f32[80,8]{1,0:T(8,128)S(1)}, f32[80,8]{1,0:T(8,128)S(1)}, u32[]{:S(2)}, u32[]{:S(2)}) collective-permute-start(f32[80,8]{1,0:T(8,128)S(1)} %get-tuple-element.129), channel_id=1, source_target_pairs={{1,0},{2,1},{3,2},{4,3},{5,4},{6,5},{7,6},{9,8},{10,9},{11,10},{12... | collective-permute-start | bytes 7688 | tf_op jit(solution)/shard_map/while/body/eval_jaxpr/ppermute | solution.py:21
  95.8 4.9 %collective-permute-start.3 = (f32[80,8]{1,0:T(8,128)S(1)}, f32[80,8]{1,0:T(8,128)S(1)}, u32[]{:S(2)}, u32[]{:S(2)}) collective-permute-start(f32[80,8]{1,0:T(8,128)S(1)} %get-tuple-element.130), channel_id=1, source_target_pairs={{0,1},{1,2},{2,3},{3,4},{4,5},{5,6},{6,7},{8,9},{9,10},{10,11},{11... | collective-permute-start | bytes 7688 | tf_op jit(solution)/shard_map/while/body/eval_jaxpr/ppermute | solution.py:20
  107.0 6.0 %collective-permute-start = (f32[8,512]{1,0:T(8,128)S(1)}, f32[8,512]{1,0:T(8,128)S(1)}, u32[]{:S(2)}, u32[]{:S(2)}) collective-permute-start(f32[8,512]{1,0:T(8,128)S(1)} %get-tuple-element.127), channel_id=1, source_target_pairs={{0,8},{8,16},{16,24},{1,9},{9,17},{17,25},{2,10},{10,18},{18,26},{... | collective-permute-start | bytes 49160 | tf_op jit(solution)/shard_map/while/body/eval_jaxpr/ppermute | solution.py:20
  111.5 5.6 %collective-permute-start.1 = (f32[8,512]{1,0:T(8,128)S(1)}, f32[8,512]{1,0:T(8,128)S(1)}, u32[]{:S(2)}, u32[]{:S(2)}) collective-permute-start(f32[8,512]{1,0:T(8,128)S(1)} %get-tuple-element.128), channel_id=1, source_target_pairs={{8,0},{16,8},{24,16},{9,1},{17,9},{25,17},{10,2},{18,10},{26,18},{... | collective-permute-start | bytes 49160 | tf_op jit(solution)/shard_map/while/body/eval_jaxpr/ppermute | solution.py:21
  128.7 4.5 %collective-permute-start = (f32[8,512]{1,0:T(8,128)S(1)}, f32[8,512]{1,0:T(8,128)S(1)}, u32[]{:S(2)}, u32[]{:S(2)}) collective-permute-start(f32[8,512]{1,0:T(8,128)S(1)} %get-tuple-element.127), channel_id=1, source_target_pairs={{0,8},{8,16},{16,24},{1,9},{9,17},{17,25},{2,10},{10,18},{18,26},{... | collective-permute-start | bytes 49160 | tf_op jit(solution)/shard_map/while/body/eval_jaxpr/ppermute | solution.py:20
  131.9 5.6 %collective-permute-start.1 = (f32[8,512]{1,0:T(8,128)S(1)}, f32[8,512]{1,0:T(8,128)S(1)}, u32[]{:S(2)}, u32[]{:S(2)}) collective-permute-start(f32[8,512]{1,0:T(8,128)S(1)} %get-tuple-element.128), channel_id=1, source_target_pairs={{8,0},{16,8},{24,16},{9,1},{17,9},{25,17},{10,2},{18,10},{26,18},{... | collective-permute-start | bytes 49160 | tf_op jit(solution)/shard_map/while/body/eval_jaxpr/ppermute | solution.py:21
  137.6 6.1 %collective-permute-start.2 = (f32[80,8]{1,0:T(8,128)S(1)}, f32[80,8]{1,0:T(8,128)S(1)}, u32[]{:S(2)}, u32[]{:S(2)}) collective-permute-start(f32[80,8]{1,0:T(8,128)S(1)} %get-tuple-element.129), channel_id=1, source_target_pairs={{1,0},{2,1},{3,2},{4,3},{5,4},{6,5},{7,6},{9,8},{10,9},{11,10},{12... | collective-permute-start | bytes 7688 | tf_op jit(solution)/shard_map/while/body/eval_jaxpr/ppermute | solution.py:21
  138.9 5.7 %collective-permute-start.3 = (f32[80,8]{1,0:T(8,128)S(1)}, f32[80,8]{1,0:T(8,128)S(1)}, u32[]{:S(2)}, u32[]{:S(2)}) collective-permute-start(f32[80,8]{1,0:T(8,128)S(1)} %get-tuple-element.130), channel_id=1, source_target_pairs={{0,1},{1,2},{2,3},{3,4},{4,5},{5,6},{6,7},{8,9},{9,10},{10,11},{11... | collective-permute-start | bytes 7688 | tf_op jit(solution)/shard_map/while/body/eval_jaxpr/ppermute | solution.py:20
  150.8 4.5 %collective-permute-start = (f32[8,512]{1,0:T(8,128)S(1)}, f32[8,512]{1,0:T(8,128)S(1)}, u32[]{:S(2)}, u32[]{:S(2)}) collective-permute-start(f32[8,512]{1,0:T(8,128)S(1)} %get-tuple-element.127), channel_id=1, source_target_pairs={{0,8},{8,16},{16,24},{1,9},{9,17},{17,25},{2,10},{10,18},{18,26},{... | collective-permute-start | bytes 49160 | tf_op jit(solution)/shard_map/while/body/eval_jaxpr/ppermute | solution.py:20
  153.9 5.6 %collective-permute-start.1 = (f32[8,512]{1,0:T(8,128)S(1)}, f32[8,512]{1,0:T(8,128)S(1)}, u32[]{:S(2)}, u32[]{:S(2)}) collective-permute-start(f32[8,512]{1,0:T(8,128)S(1)} %get-tuple-element.128), channel_id=1, source_target_pairs={{8,0},{16,8},{24,16},{9,1},{17,9},{25,17},{10,2},{18,10},{26,18},{... | collective-permute-start | bytes 49160 | tf_op jit(solution)/shard_map/while/body/eval_jaxpr/ppermute | solution.py:21
  159.6 6.1 %collective-permute-start.2 = (f32[80,8]{1,0:T(8,128)S(1)}, f32[80,8]{1,0:T(8,128)S(1)}, u32[]{:S(2)}, u32[]{:S(2)}) collective-permute-start(f32[80,8]{1,0:T(8,128)S(1)} %get-tuple-element.129), channel_id=1, source_target_pairs={{1,0},{2,1},{3,2},{4,3},{5,4},{6,5},{7,6},{9,8},{10,9},{11,10},{12... | collective-permute-start | bytes 7688 | tf_op jit(solution)/shard_map/while/body/eval_jaxpr/ppermute | solution.py:21
  160.9 5.7 %collective-permute-start.3 = (f32[80,8]{1,0:T(8,128)S(1)}, f32[80,8]{1,0:T(8,128)S(1)}, u32[]{:S(2)}, u32[]{:S(2)}) collective-permute-start(f32[80,8]{1,0:T(8,128)S(1)} %get-tuple-element.130), channel_id=1, source_target_pairs={{0,1},{1,2},{2,3},{3,4},{4,5},{5,6},{6,7},{8,9},{9,10},{10,11},{11... | collective-permute-start | bytes 7688 | tf_op jit(solution)/shard_map/while/body/eval_jaxpr/ppermute | solution.py:20
  172.9 4.5 %collective-permute-start = (f32[8,512]{1,0:T(8,128)S(1)}, f32[8,512]{1,0:T(8,128)S(1)}, u32[]{:S(2)}, u32[]{:S(2)}) collective-permute-start(f32[8,512]{1,0:T(8,128)S(1)} %get-tuple-element.127), channel_id=1, source_target_pairs={{0,8},{8,16},{16,24},{1,9},{9,17},{17,25},{2,10},{10,18},{18,26},{... | collective-permute-start | bytes 49160 | tf_op jit(solution)/shard_map/while/body/eval_jaxpr/ppermute | solution.py:20
  176.0 5.6 %collective-permute-start.1 = (f32[8,512]{1,0:T(8,128)S(1)}, f32[8,512]{1,0:T(8,128)S(1)}, u32[]{:S(2)}, u32[]{:S(2)}) collective-permute-start(f32[8,512]{1,0:T(8,128)S(1)} %get-tuple-element.128), channel_id=1, source_target_pairs={{8,0},{16,8},{24,16},{9,1},{17,9},{25,17},{10,2},{18,10},{26,18},{... | collective-permute-start | bytes 49160 | tf_op jit(solution)/shard_map/while/body/eval_jaxpr/ppermute | solution.py:21
  181.7 6.1 %collective-permute-start.2 = (f32[80,8]{1,0:T(8,128)S(1)}, f32[80,8]{1,0:T(8,128)S(1)}, u32[]{:S(2)}, u32[]{:S(2)}) collective-permute-start(f32[80,8]{1,0:T(8,128)S(1)} %get-tuple-element.129), channel_id=1, source_target_pairs={{1,0},{2,1},{3,2},{4,3},{5,4},{6,5},{7,6},{9,8},{10,9},{11,10},{12... | collective-permute-start | bytes 7688 | tf_op jit(solution)/shard_map/while/body/eval_jaxpr/ppermute | solution.py:21
  183.0 5.7 %collective-permute-start.3 = (f32[80,8]{1,0:T(8,128)S(1)}, f32[80,8]{1,0:T(8,128)S(1)}, u32[]{:S(2)}, u32[]{:S(2)}) collective-permute-start(f32[80,8]{1,0:T(8,128)S(1)} %get-tuple-element.130), channel_id=1, source_target_pairs={{0,1},{1,2},{2,3},{3,4},{4,5},{5,6},{6,7},{8,9},{9,10},{10,11},{11... | collective-permute-start | bytes 7688 | tf_op jit(solution)/shard_map/while/body/eval_jaxpr/ppermute | solution.py:20
  194.9 4.5 %collective-permute-start = (f32[8,512]{1,0:T(8,128)S(1)}, f32[8,512]{1,0:T(8,128)S(1)}, u32[]{:S(2)}, u32[]{:S(2)}) collective-permute-start(f32[8,512]{1,0:T(8,128)S(1)} %get-tuple-element.127), channel_id=1, source_target_pairs={{0,8},{8,16},{16,24},{1,9},{9,17},{17,25},{2,10},{10,18},{18,26},{... | collective-permute-start | bytes 49160 | tf_op jit(solution)/shard_map/while/body/eval_jaxpr/ppermute | solution.py:20
  198.0 5.6 %collective-permute-start.1 = (f32[8,512]{1,0:T(8,128)S(1)}, f32[8,512]{1,0:T(8,128)S(1)}, u32[]{:S(2)}, u32[]{:S(2)}) collective-permute-start(f32[8,512]{1,0:T(8,128)S(1)} %get-tuple-element.128), channel_id=1, source_target_pairs={{8,0},{16,8},{24,16},{9,1},{17,9},{25,17},{10,2},{18,10},{26,18},{... | collective-permute-start | bytes 49160 | tf_op jit(solution)/shard_map/while/body/eval_jaxpr/ppermute | solution.py:21
  203.7 6.1 %collective-permute-start.2 = (f32[80,8]{1,0:T(8,128)S(1)}, f32[80,8]{1,0:T(8,128)S(1)}, u32[]{:S(2)}, u32[]{:S(2)}) collective-permute-start(f32[80,8]{1,0:T(8,128)S(1)} %get-tuple-element.129), channel_id=1, source_target_pairs={{1,0},{2,1},{3,2},{4,3},{5,4},{6,5},{7,6},{9,8},{10,9},{11,10},{12... | collective-permute-start | bytes 7688 | tf_op jit(solution)/shard_map/while/body/eval_jaxpr/ppermute | solution.py:21
  205.0 5.7 %collective-permute-start.3 = (f32[80,8]{1,0:T(8,128)S(1)}, f32[80,8]{1,0:T(8,128)S(1)}, u32[]{:S(2)}, u32[]{:S(2)}) collective-permute-start(f32[80,8]{1,0:T(8,128)S(1)} %get-tuple-element.130), channel_id=1, source_target_pairs={{0,1},{1,2},{2,3},{3,4},{4,5},{5,6},{6,7},{8,9},{9,10},{10,11},{11... | collective-permute-start | bytes 7688 | tf_op jit(solution)/shard_map/while/body/eval_jaxpr/ppermute | solution.py:20
  220.1 5.6 %collective-permute-start.1 = (f32[8,512]{1,0:T(8,128)S(1)}, f32[8,512]{1,0:T(8,128)S(1)}, u32[]{:S(2)}, u32[]{:S(2)}) collective-permute-start(f32[8,512]{1,0:T(8,128)S(1)} %get-tuple-element.128), channel_id=1, source_target_pairs={{8,0},{16,8},{24,16},{9,1},{17,9},{25,17},{10,2},{18,10},{26,18},{... | collective-permute-start | bytes 49160 | tf_op jit(solution)/shard_map/while/body/eval_jaxpr/ppermute | solution.py:21
  225.8 6.1 %collective-permute-start.2 = (f32[80,8]{1,0:T(8,128)S(1)}, f32[80,8]{1,0:T(8,128)S(1)}, u32[]{:S(2)}, u32[]{:S(2)}) collective-permute-start(f32[80,8]{1,0:T(8,128)S(1)} %get-tuple-element.129), channel_id=1, source_target_pairs={{1,0},{2,1},{3,2},{4,3},{5,4},{6,5},{7,6},{9,8},{10,9},{11,10},{12... | collective-permute-start | bytes 7688 | tf_op jit(solution)/shard_map/while/body/eval_jaxpr/ppermute | solution.py:21
  227.1 5.7 %collective-permute-start.3 = (f32[80,8]{1,0:T(8,128)S(1)}, f32[80,8]{1,0:T(8,128)S(1)}, u32[]{:S(2)}, u32[]{:S(2)}) collective-permute-start(f32[80,8]{1,0:T(8,128)S(1)} %get-tuple-element.130), channel_id=1, source_target_pairs={{0,1},{1,2},{2,3},{3,4},{4,5},{5,6},{6,7},{8,9},{9,10},{10,11},{11... | collective-permute-start | bytes 7688 | tf_op jit(solution)/shard_map/while/body/eval_jaxpr/ppermute | solution.py:20
  242.1 5.6 %collective-permute-start.1 = (f32[8,512]{1,0:T(8,128)S(1)}, f32[8,512]{1,0:T(8,128)S(1)}, u32[]{:S(2)}, u32[]{:S(2)}) collective-permute-start(f32[8,512]{1,0:T(8,128)S(1)} %get-tuple-element.128), channel_id=1, source_target_pairs={{8,0},{16,8},{24,16},{9,1},{17,9},{25,17},{10,2},{18,10},{26,18},{... | collective-permute-start | bytes 49160 | tf_op jit(solution)/shard_map/while/body/eval_jaxpr/ppermute | solution.py:21
  247.9 6.1 %collective-permute-start.2 = (f32[80,8]{1,0:T(8,128)S(1)}, f32[80,8]{1,0:T(8,128)S(1)}, u32[]{:S(2)}, u32[]{:S(2)}) collective-permute-start(f32[80,8]{1,0:T(8,128)S(1)} %get-tuple-element.129), channel_id=1, source_target_pairs={{1,0},{2,1},{3,2},{4,3},{5,4},{6,5},{7,6},{9,8},{10,9},{11,10},{12... | collective-permute-start | bytes 7688 | tf_op jit(solution)/shard_map/while/body/eval_jaxpr/ppermute | solution.py:21
  249.2 5.7 %collective-permute-start.3 = (f32[80,8]{1,0:T(8,128)S(1)}, f32[80,8]{1,0:T(8,128)S(1)}, u32[]{:S(2)}, u32[]{:S(2)}) collective-permute-start(f32[80,8]{1,0:T(8,128)S(1)} %get-tuple-element.130), channel_id=1, source_target_pairs={{0,1},{1,2},{2,3},{3,4},{4,5},{5,6},{6,7},{8,9},{9,10},{10,11},{11... | collective-permute-start | bytes 7688 | tf_op jit(solution)/shard_map/while/body/eval_jaxpr/ppermute | solution.py:20
  (11 other events, 36.1 us)
where the time goes:
time: 267 us; the launch traced here: 262 us
  starting transfers between devices  148 us (55%)
  waiting for transfers between devices  56.4 us (21%)
  other arithmetic  54.4 us (20%)
    ppermute x28, starting transfers between devices, extended(): before = lax.ppermute(last, axis, up)  112 us
    ppermute x28, waiting for transfers between devices, extended(): after = lax.ppermute(initial, axis, down)  48 us
    select_n x64, other arithmetic, group_pass(): sent = jnp.where(route_here > 0, current, jnp.float32(0.0))  45.4 us
    ppermute x28, starting transfers between devices, extended(): after = lax.ppermute(initial, axis, down)  36.1 us
    ppermute x28, waiting for transfers between devices, extended(): before = lax.ppermute(last, axis, up)  8.41 us
  transfers between devices with their start and end apart: 56, of which 30 were waited for; matrix products, arithmetic and copies ran while one was open for 0% of the time, Pallas kernels for 0%

commit v1 on v0

v1 whole, which is shorter than its diff:
```python
import functools

import jax
import jax.numpy as jnp
from jax import lax
from jax.experimental import pallas as pl
from jax.experimental.pallas import tpu as pltpu
from jax.sharding import PartitionSpec as P

SUBSTEPS = 3
PASSES = 64
OFFSETS = ((0, 1), (1, 1), (1, 0), (1, -1), (0, -1), (-1, -1), (-1, 0), (-1, 1))
LANES = 128
SUB = 8
MARGIN = 24
GROUPS = (20, 22, 22)
MESH = pl.DeviceIdType.MESH


def kernel(
    row_peers, col_peers,
    depth_ref, rain_ref, conv_ref, dir_ref, outlet_ref,
    level_ref, discharge_ref,
    depth_ext, rain_ext, coef_ext, route_ext, acc_ext, plain,
    acc, rain, coef, level, share, masks,
    send_sem, recv_sem,
):
    rows, cols = depth_ref.shape
    total = rows + 2 * MARGIN
    bands = total // SUB
    wide = cols + LANES
    own = cols // LANES
    my_row, my_col = lax.axis_index("row"), lax.axis_index("col")

    def exists(dr, dc):
        r, c = my_row + dr, my_col + dc
        ok = None
        for test in ((r >= 0, r < row_peers) if dr else ()) + ((c >= 0, c < col_peers) if dc else ()):
            ok = test if ok is None else jnp.logical_and(ok, test)
        return ok

    def row_place(dr):
        if dr == 0:
            return (pl.ds(0, rows), pl.ds(0, rows))
        if dr < 0:
            return (pl.ds(0, MARGIN), pl.ds(rows, MARGIN))
        return (pl.ds(rows - MARGIN, MARGIN), pl.ds(rows + MARGIN, MARGIN))

    def col_place(dc):
        if dc == 0:
            return (pl.ds(0, own), pl.ds(0, own))
        if dc < 0:
            return (pl.ds(0, 1), pl.ds(own, 1))
        return (pl.ds(own - 1, 1), pl.ds(own + 1, 1))

    def copy(slot, k, src, dst):
        dr, dc = OFFSETS[k]
        (rs, rd), (cs, cd) = row_place(dr), col_place(dc)
        return pltpu.make_async_remote_copy(
            src_ref=src.at[cs, rs],
            dst_ref=dst.at[cd, rd],
            send_sem=send_sem.at[slot, k],
            recv_sem=recv_sem.at[slot, k],
            device_id=(my_row + dr, my_col + dc),
            device_id_type=MESH,
        )

    order = (1, 3, 5, 7, 2, 6, 0, 4)

    def send(slot, src, dst):
        for k in order:
            @pl.when(exists(*OFFSETS[k]))
            def _(k=k):
                copy(slot, k, src, dst).start()

    def receive(slot, src, dst):
        for k in order:
            dr, dc = OFFSETS[k]
            there = exists(-dr, -dc)

            @pl.when(there)
            def _(k=k):
                copy(slot, k, src, dst).wait_recv()

            @pl.when(jnp.logical_not(there))
            def _(dr=dr, dc=dc):
                _, rd = row_place(dr)
                _, cd = col_place(dc)
                dst[cd, rd] = jnp.zeros((cd.size, rd.size, LANES), dst.dtype)

    def sent_out(slot, src, dst):
        for k in order:
            @pl.when(exists(*OFFSETS[k]))
            def _(k=k):
                copy(slot, k, src, dst).wait_send()

    barrier = pltpu.get_barrier_semaphore()
    for dr, dc in OFFSETS:
        @pl.when(exists(dr, dc))
        def _(dr=dr, dc=dc):
            pl.semaphore_signal(
                barrier, inc=1, device_id=(my_row + dr, my_col + dc), device_id_type=MESH
            )
    for c in range(own):
        at = pl.ds(c * LANES, LANES)
        mine = pl.ds(0, rows)
        depth_ext[c, mine] = depth_ref[:, at]
        rain_ext[c, mine] = rain_ref[:, at]
        code = dir_ref[:, at]
        route_ext[c, mine] = jnp.where(outlet_ref[:, at] == 1, 0, code + 1)
        coef_ext[c, mine] = conv_ref[:, at] * jnp.where(
            (code & 1) == 1, jnp.float32(0.70710678), jnp.float32(1.0)
        )
    def reach(index, peers):
        return 1 + jnp.where(index > 0, 1, 0) + jnp.where(index < peers - 1, 1, 0)

    pl.semaphore_wait(barrier, reach(my_row, row_peers) * reach(my_col, col_peers) - 1)

    firsts = (depth_ext, coef_ext, rain_ext, route_ext)
    for slot, ext in enumerate(firsts):
        send(slot, ext, ext)
    for slot, ext in enumerate(firsts):
        receive(slot, ext, ext)

    right = lax.broadcasted_iota(jnp.int32, (SUB, LANES), 1) < LANES // 2

    def banded(ext, v):
        def part(c):
            return ext[c, pl.ds(v, SUB, stride=bands), :]

        blocks = [part(c) for c in range(own)]
        blocks.append(jnp.where(right, part(own), part(own + 1)))
        return jnp.concatenate(blocks, axis=1)

    for v in range(bands):
        acc[v] = banded(depth_ext, v)
        rain[v] = banded(rain_ext, v)
        coef[v] = banded(coef_ext, v)

    def above(v, get):
        return get(v - 1) if v else pltpu.roll(get(bands - 1), 1, 0)

    def below(v, get):
        return get(v + 1) if v < bands - 1 else pltpu.roll(get(0), SUB - 1, 0)

    def routed(v):
        return banded(route_ext, v)

    for v in range(bands):
        near = {1: above(v, routed), 0: routed(v), -1: below(v, routed)}
        for k, (di, dj) in enumerate(OFFSETS):
            masks[k, v] = jnp.where(near[di] == k + 1, jnp.float32(1.0), jnp.float32(0.0))

    def inflow(v, up, here, down):
        near = {1: up, 0: here, -1: down}
        parts = {}
        for k, (di, dj) in enumerate(OFFSETS):
            term = masks[k, v] * near[di]
            parts[dj] = parts[dj] + term if dj in parts else term
        return parts[0] + (pltpu.roll(parts[1], 1, 1) + pltpu.roll(parts[-1], wide - 1, 1))

    def sweep(field, finish):
        start = field[0]
        up, here = (pltpu.roll(field[bands - 1], 1, 0), start)
        for v in range(bands):
            down = field[v + 1] if v < bands - 1 else pltpu.roll(start, SUB - 1, 0)
            finish(v, inflow(v, up, here, down))
            up, here = here, down

    @pl.loop(0, SUBSTEPS)
    def _(step):
        for v in range(bands):
            h = acc[v]
            factor = coef[v] * jnp.exp(jnp.log(h) * jnp.float32(2.0 / 3.0))
            out = h * (factor / (1.0 + factor))
            share[v] = out
            level[v] = h + rain[v] - out

        def finish(v, came):
            acc[v] = level[v] + came

        sweep(share, finish)

    for v in range(bands):
        level[v] = acc[v]

    def finish(v, came):
        acc[v] = level[v] + came

    def passes(count):
        @pl.loop(0, count)
        def _(index):
            sweep(acc, finish)

    def to_plain(field, dst):
        for v in range(bands):
            value = field[v]
            for c in range(own):
                dst[c, pl.ds(v, SUB, stride=bands), :] = value[:, c * LANES : (c + 1) * LANES]

    passes(GROUPS[0])
    to_plain(level, plain.at[len(GROUPS) - 1])
    for c in range(own):
        level_ref[:, pl.ds(c * LANES, LANES)] = plain[len(GROUPS) - 1, c, pl.ds(0, rows), :]
    sub = lax.broadcasted_iota(jnp.int32, (SUB, LANES), 0)
    for group in range(1, len(GROUPS)):
        slot = len(firsts) + group - 1
        src, dst = plain.at[group - 1], acc_ext.at[group - 1]
        to_plain(acc, src)
        send(slot, src, dst)
        receive(slot, src, dst)
        for v in range(bands):
            inner = sub * bands + v < rows
            for c in range(own):
                at = pl.ds(c * LANES, LANES)
                acc[v, :, at] = jnp.where(
                    inner, acc[v, :, at], dst[c, pl.ds(v, SUB, stride=bands), :]
                )
            acc[v, :, pl.ds(cols, LANES)] = jnp.where(
                right,
                dst[own, pl.ds(v, SUB, stride=bands), :],
                dst[own + 1, pl.ds(v, SUB, stride=bands), :],
            )
        passes(GROUPS[group])

    to_plain(acc, plain.at[len(GROUPS)])
    for c in range(own):
        discharge_ref[:, pl.ds(c * LANES, LANES)] = jnp.log(
            1.0 + plain[len(GROUPS), c, pl.ds(0, rows), :]
        )
    for slot, ext in enumerate(firsts):
        sent_out(slot, ext, ext)
    for group in range(1, len(GROUPS)):
        sent_out(len(firsts) + group - 1, plain.at[group - 1], acc_ext.at[group - 1])


def solution(mesh):
    row_peers, col_peers = mesh.shape["row"], mesh.shape["col"]

    def on_device(depth, rainfall, conveyance, flow_dir, outlet):
        rows, cols = depth.shape
        total = rows + 2 * MARGIN
        bands = total // SUB
        wide = cols + LANES
        slots = 4 + len(GROUPS) - 1
        own = cols // LANES
        ext = (own + 2, total, LANES)
        field = (bands, SUB, wide)
        vmem = pl.BlockSpec(memory_space=pltpu.VMEM)
        f32 = jnp.float32
        return pl.pallas_call(
            functools.partial(kernel, row_peers, col_peers),
            out_shape=(jax.ShapeDtypeStruct((rows, cols), f32),) * 2,
            in_specs=[vmem] * 5,
            out_specs=(vmem, vmem),
            scratch_shapes=[
                pltpu.VMEM(ext, f32),
                pltpu.VMEM(ext, f32),
                pltpu.VMEM(ext, f32),
                pltpu.VMEM(ext, jnp.int32),
                pltpu.VMEM((len(GROUPS) - 1,) + ext, f32),
                pltpu.VMEM((len(GROUPS) + 1, own, total, LANES), f32),
                pltpu.VMEM(field, f32),
                pltpu.VMEM(field, f32),
                pltpu.VMEM(field, f32),
                pltpu.VMEM(field, f32),
                pltpu.VMEM(field, f32),
                pltpu.VMEM((len(OFFSETS),) + field, f32),
                pltpu.SemaphoreType.DMA((slots, len(OFFSETS))),
                pltpu.SemaphoreType.DMA((slots, len(OFFSETS))),
            ],
            compiler_params=pltpu.CompilerParams(collective_id=0, has_side_effects=True),
        )(depth, rainfall, conveyance, flow_dir, outlet)

    placed = P("row", "col")
    return jax.shard_map(
        on_device,
        mesh=mesh,
        in_specs=(placed,) * 5,
        out_specs=(placed, placed),
        check_vma=False,
    )
```

time: 267 us -> 49.2 us (0.18); the launches traced: 262 us -> 49.1 us
  starting transfers between devices: 148 us -> 0 us
  waiting for transfers between devices: 56.4 us -> 0 us
  other arithmetic: 54.4 us -> 0 us
  Pallas kernels: 0 us -> 46.2 us
    ppermute x56 -> x0, starting transfers between devices: 148 us -> none  [the longest x28 112 us: extended(): before = lax.ppermute(last, axis, up)]
    ppermute x56 -> x0, waiting for transfers between devices: 56.4 us -> none  [the longest x28 48 us: extended(): after = lax.ppermute(initial, axis, down)]
    select_n x67 -> x0, other arithmetic: 48.1 us -> none  [the longest x64 45.4 us: group_pass(): sent = jnp.where(route_here > 0, current, jnp.float32(0.0))]
    pallas_call x0 -> x1, Pallas kernels: none -> 46.2 us  [on_device(): pl.pallas_call(functools.partial(kernel, row_peers, col_peers), out_shape...]
    add x9 -> x0, other arithmetic: 4.46 us -> none  [the longest x8 4.06 us: group_pass(): current = level_here + padded_inflow(sent, route_here)]
  transfers between devices with their start and end apart: 56 -> 0, of which waited for: 30 -> 0; matrix products, arithmetic and copies ran while one was open for 0% -> 0% of each run, Pallas kernels for 0% -> 0%
where the time goes in v1:
time: 49.2 us; the launch traced here: 49.1 us
  Pallas kernels  46.2 us (94%)
  local copies, waits for them, and re-layouts  2.26 us (5%)
  between operations  0.65 us (1%)
    pallas_call x1, Pallas kernels, on_device(): pl.pallas_call(functools.partial(kernel, row_peers, col_peers), out_shape...  46.2 us
    unnamed x4, local copies, waits for them, and re-layouts  2.26 us

profile of v1, /device:TPU:0, one launch (start us, length us, event | category | flops | bytes accessed | tf_op | source)
XLA Modules:
  0.0 49.1 jit_solution(7781494540854697458)
XLA Ops:
  0.6 46.2 %shard_map.68 = (f32[64,512]{1,0:T(8,128)}, f32[64,512]{1,0:T(8,128)}) custom-call(f32[64,512]{1,0:T(8,128)} %depth_ref.1, f32[64,512]{1,0:T(8,128)} %rain_ref.1, f32[64,512]{1,0:T(8,128)} %conv_ref.1, s32[64,512]{1,0:T(8,128)} %dir_ref.1, s32[64,512]{1,0:T(8,128)} %outlet_ref.1), custom_call_target="tpu_custom_call" | custom-call | tf_op jit(solution)/shard_map/pallas_call | solution.py:251
  46.8 0.0 copy-start
  46.8 1.6 %copy.9 = f32[64,512]{1,0:T(8,128)} copy(f32[64,512]{1,0:T(8,128)} %get-tuple-element.4) | data formatting | bytes 262144
  48.4 0.0 copy-done
  48.4 0.7 %copy.10 = f32[64,512]{1,0:T(8,128)} copy(f32[64,512]{1,0:T(8,128)S(1)} %copy-done) | data formatting | bytes 262144
Async XLA Ops:
  46.8 1.6 %copy-start = (f32[64,512]{1,0:T(8,128)S(1)}, f32[64,512]{1,0:T(8,128)}, u32[]{:S(2)}) copy-start(f32[64,512]{1,0:T(8,128)} %get-tuple-element.5) | copy-start | bytes 393220

commit v2 on v1

--- a/solution.py
+++ b/solution.py
@@ -12,8 +12,10 @@
 OFFSETS = ((0, 1), (1, 1), (1, 0), (1, -1), (0, -1), (-1, -1), (-1, 0), (-1, 1))
 LANES = 128
 SUB = 8
-MARGIN = 24
-GROUPS = (20, 22, 22)
+NEAR = 8
+MARGIN = 32
+GROUPS = PASSES // MARGIN
+SPARE = 0
 MESH = pl.DeviceIdType.MESH
 
 
@@ -21,12 +23,12 @@
     row_peers, col_peers,
     depth_ref, rain_ref, conv_ref, dir_ref, outlet_ref,
     level_ref, discharge_ref,
-    depth_ext, rain_ext, coef_ext, route_ext, acc_ext, plain,
+    depth_ext, rain_ext, coef_ext, route_ext, far_ext, acc_ext, plain,
     acc, rain, coef, level, share, masks,
     send_sem, recv_sem,
 ):
     rows, cols = depth_ref.shape
-    total = rows + 2 * MARGIN
+    total = depth_ext.shape[1]
     bands = total // SUB
     wide = cols + LANES
     own = cols // LANES
@@ -39,12 +41,12 @@
             ok = test if ok is None else jnp.logical_and(ok, test)
         return ok
 
-    def row_place(dr):
+    def row_place(dr, width):
         if dr == 0:
             return (pl.ds(0, rows), pl.ds(0, rows))
         if dr < 0:
-            return (pl.ds(0, MARGIN), pl.ds(rows, MARGIN))
-        return (pl.ds(rows - MARGIN, MARGIN), pl.ds(rows + MARGIN, MARGIN))
+            return (pl.ds(0, width), pl.ds(rows, width))
+        return (pl.ds(rows - width, width), pl.ds(total - width, width))
 
     def col_place(dc):
         if dc == 0:
@@ -53,9 +55,9 @@
             return (pl.ds(0, 1), pl.ds(own, 1))
         return (pl.ds(own - 1, 1), pl.ds(own + 1, 1))
 
-    def copy(slot, k, src, dst):
+    def copy(slot, k, src, dst, width):
         dr, dc = OFFSETS[k]
-        (rs, rd), (cs, cd) = row_place(dr), col_place(dc)
+        (rs, rd), (cs, cd) = row_place(dr, width), col_place(dc)
         return pltpu.make_async_remote_copy(
             src_ref=src.at[cs, rs],
             dst_ref=dst.at[cd, rd],
@@ -65,34 +67,35 @@
             device_id_type=MESH,
         )
 
-    order = (1, 3, 5, 7, 2, 6, 0, 4)
-
-    def send(slot, src, dst):
+    every = (1, 3, 5, 7, 2, 6, 0, 4)
+    slanted = (1, 3, 5, 7, 2, 6)
+
+    def send(slot, src, dst, width, order=every):
         for k in order:
             @pl.when(exists(*OFFSETS[k]))
             def _(k=k):
-                copy(slot, k, src, dst).start()
-
-    def receive(slot, src, dst):
+                copy(slot, k, src, dst, width).start()
+
+    def receive(slot, src, dst, width, order=every):
         for k in order:
             dr, dc = OFFSETS[k]
             there = exists(-dr, -dc)
 
             @pl.when(there)
             def _(k=k):
-                copy(slot, k, src, dst).wait_recv()
+                copy(slot, k, src, dst, width).wait_recv()
 
             @pl.when(jnp.logical_not(there))
             def _(dr=dr, dc=dc):
-                _, rd = row_place(dr)
+                _, rd = row_place(dr, width)
                 _, cd = col_place(dc)
                 dst[cd, rd] = jnp.zeros((cd.size, rd.size, LANES), dst.dtype)
 
-    def sent_out(slot, src, dst):
+    def sent_out(slot, src, dst, width, order=every):
         for k in order:
             @pl.when(exists(*OFFSETS[k]))
             def _(k=k):
-                copy(slot, k, src, dst).wait_send()
+                copy(slot, k, src, dst, width).wait_send()
 
     barrier = pltpu.get_barrier_semaphore()
     for dr, dc in OFFSETS:
@@ -107,7 +110,9 @@
         depth_ext[c, mine] = depth_ref[:, at]
         rain_ext[c, mine] = rain_ref[:, at]
         code = dir_ref[:, at]
-        route_ext[c, mine] = jnp.where(outlet_ref[:, at] == 1, 0, code + 1)
+        route = jnp.where(outlet_ref[:, at] == 1, 0, code + 1)
+        route_ext[c, mine] = route
+        far_ext[c, mine] = route
         coef_ext[c, mine] = conv_ref[:, at] * jnp.where(
             (code & 1) == 1, jnp.float32(0.70710678), jnp.float32(1.0)
         )
@@ -117,10 +122,20 @@
     pl.semaphore_wait(barrier, reach(my_row, row_peers) * reach(my_col, col_peers) - 1)
 
     firsts = (depth_ext, coef_ext, rain_ext, route_ext)
+    far_slot, level_slot = (len(firsts), len(firsts) + 1)
     for slot, ext in enumerate(firsts):
-        send(slot, ext, ext)
+        send(slot, ext, ext, NEAR)
+    send(far_slot, far_ext, far_ext, MARGIN, slanted)
+    unused = pl.ds(rows + NEAR, total - rows - 2 * NEAR)
+    for ext in firsts:
+        ext[:, unused] = jnp.zeros((own + 2, total - rows - 2 * NEAR, LANES), ext.dtype)
+    if SPARE:
+        for ext in (far_ext,) + tuple(acc_ext.at[g] for g in range(GROUPS)):
+            ext[:, pl.ds(rows + MARGIN, SPARE)] = jnp.zeros((own + 2, SPARE, LANES), ext.dtype)
     for slot, ext in enumerate(firsts):
-        receive(slot, ext, ext)
+        receive(slot, ext, ext, NEAR)
+    sides = (pl.ds(own, 2), pl.ds(0, rows))
+    far_ext[sides] = route_ext[sides]
 
     right = lax.broadcasted_iota(jnp.int32, (SUB, LANES), 1) < LANES // 2
 
@@ -143,13 +158,16 @@
     def below(v, get):
         return get(v + 1) if v < bands - 1 else pltpu.roll(get(0), SUB - 1, 0)
 
-    def routed(v):
-        return banded(route_ext, v)
-
-    for v in range(bands):
-        near = {1: above(v, routed), 0: routed(v), -1: below(v, routed)}
-        for k, (di, dj) in enumerate(OFFSETS):
-            masks[k, v] = jnp.where(near[di] == k + 1, jnp.float32(1.0), jnp.float32(0.0))
+    def set_masks(ext):
+        def routed(v):
+            return banded(ext, v)
+
+        for v in range(bands):
+            near = {1: above(v, routed), 0: routed(v), -1: below(v, routed)}
+            for k, (di, dj) in enumerate(OFFSETS):
+                masks[k, v] = jnp.where(near[di] == k + 1, jnp.float32(1.0), jnp.float32(0.0))
+
+    set_masks(route_ext)
 
     def inflow(v, up, here, down):
         near = {1: up, 0: here, -1: down}
@@ -181,9 +199,6 @@
 
         sweep(share, finish)
 
-    for v in range(bands):
-        level[v] = acc[v]
-
     def finish(v, came):
         acc[v] = level[v] + came
 
@@ -198,40 +213,48 @@
             for c in range(own):
                 dst[c, pl.ds(v, SUB, stride=bands), :] = value[:, c * LANES : (c + 1) * LANES]
 
-    passes(GROUPS[0])
-    to_plain(level, plain.at[len(GROUPS) - 1])
-    for c in range(own):
-        level_ref[:, pl.ds(c * LANES, LANES)] = plain[len(GROUPS) - 1, c, pl.ds(0, rows), :]
     sub = lax.broadcasted_iota(jnp.int32, (SUB, LANES), 0)
-    for group in range(1, len(GROUPS)):
-        slot = len(firsts) + group - 1
-        src, dst = plain.at[group - 1], acc_ext.at[group - 1]
+
+    def widen(src, dst, slot, meanwhile, fields):
         to_plain(acc, src)
-        send(slot, src, dst)
-        receive(slot, src, dst)
+        send(slot, src, dst, MARGIN)
+        meanwhile()
+        receive(slot, src, dst, MARGIN)
         for v in range(bands):
             inner = sub * bands + v < rows
             for c in range(own):
                 at = pl.ds(c * LANES, LANES)
-                acc[v, :, at] = jnp.where(
-                    inner, acc[v, :, at], dst[c, pl.ds(v, SUB, stride=bands), :]
-                )
-            acc[v, :, pl.ds(cols, LANES)] = jnp.where(
+                value = jnp.where(inner, acc[v, :, at], dst[c, pl.ds(v, SUB, stride=bands), :])
+                for field in fields:
+                    field[v, :, at] = value
+            value = jnp.where(
                 right,
                 dst[own, pl.ds(v, SUB, stride=bands), :],
                 dst[own + 1, pl.ds(v, SUB, stride=bands), :],
             )
-        passes(GROUPS[group])
-
-    to_plain(acc, plain.at[len(GROUPS)])
+            for field in fields:
+                field[v, :, pl.ds(cols, LANES)] = value
+
+    def in_flight():
+        for c in range(own):
+            level_ref[:, pl.ds(c * LANES, LANES)] = plain[0, c, pl.ds(0, rows), :]
+        receive(far_slot, far_ext, far_ext, MARGIN, slanted)
+        set_masks(far_ext)
+
+    widen(plain.at[0], acc_ext.at[0], level_slot, in_flight, (acc, level))
+    passes(MARGIN)
+    for group in range(1, GROUPS):
+        widen(plain.at[group], acc_ext.at[group], level_slot + group, lambda: None, (acc,))
+        passes(MARGIN)
+
+    to_plain(acc, plain.at[GROUPS])
     for c in range(own):
-        discharge_ref[:, pl.ds(c * LANES, LANES)] = jnp.log(
-            1.0 + plain[len(GROUPS), c, pl.ds(0, rows), :]
-        )
+        discharge_ref[:, pl.ds(c * LANES, LANES)] = jnp.log(1.0 + plain[GROUPS, c, pl.ds(0, rows), :])
     for slot, ext in enumerate(firsts):
-        sent_out(slot, ext, ext)
-    for group in range(1, len(GROUPS)):
-        sent_out(len(firsts) + group - 1, plain.at[group - 1], acc_ext.at[group - 1])
+        sent_out(slot, ext, ext, NEAR)
+    sent_out(far_slot, far_ext, far_ext, MARGIN, slanted)
+    for group in range(GROUPS):
+        sent_out(level_slot + group, plain.at[group], acc_ext.at[group], MARGIN)
 
 
 def solution(mesh):
@@ -239,10 +262,10 @@
 
     def on_device(depth, rainfall, conveyance, flow_dir, outlet):
         rows, cols = depth.shape
-        total = rows + 2 * MARGIN
+        total = rows + 2 * MARGIN + SPARE
         bands = total // SUB
         wide = cols + LANES
-        slots = 4 + len(GROUPS) - 1
+        slots = 5 + GROUPS
         own = cols // LANES
         ext = (own + 2, total, LANES)
         field = (bands, SUB, wide)
@@ -258,8 +281,9 @@
                 pltpu.VMEM(ext, f32),
                 pltpu.VMEM(ext, f32),
                 pltpu.VMEM(ext, jnp.int32),
-                pltpu.VMEM((len(GROUPS) - 1,) + ext, f32),
-                pltpu.VMEM((len(GROUPS) + 1, own, total, LANES), f32),
+                pltpu.VMEM(ext, jnp.int32),
+                pltpu.VMEM((GROUPS,) + ext, f32),
+                pltpu.VMEM((GROUPS + 1, own, total, LANES), f32),
                 pltpu.VMEM(field, f32),
                 pltpu.VMEM(field, f32),
                 pltpu.VMEM(field, f32),

time: 49.2 us -> 47.1 us (0.957)
  Pallas kernels: 46.2 us -> 44 us
    pallas_call x1, Pallas kernels: 46.2 us -> 44 us  [on_device(): pl.pallas_call(functools.partial(kernel, row_peers, col_peers), out_shape...]
where the time goes in v2:
time: 47.1 us; the launch traced here: 47 us
  Pallas kernels  44 us (93%)
  local copies, waits for them, and re-layouts  2.26 us (5%)
  between operations  0.65 us (1%)
    pallas_call x1, Pallas kernels, on_device(): pl.pallas_call(functools.partial(kernel, row_peers, col_peers), out_shape...  44 us
    unnamed x4, local copies, waits for them, and re-layouts  2.26 us

profile of v2, /device:TPU:0, one launch (start us, length us, event | category | flops | bytes accessed | tf_op | source)
XLA Modules:
  0.0 47.0 jit_solution(5245094045911032048)
XLA Ops:
  0.6 44.0 %shard_map.68 = (f32[64,512]{1,0:T(8,128)}, f32[64,512]{1,0:T(8,128)}) custom-call(f32[64,512]{1,0:T(8,128)} %depth_ref.1, f32[64,512]{1,0:T(8,128)} %rain_ref.1, f32[64,512]{1,0:T(8,128)} %conv_ref.1, s32[64,512]{1,0:T(8,128)} %dir_ref.1, s32[64,512]{1,0:T(8,128)} %outlet_ref.1), custom_call_target="tpu_custom_call" | custom-call | tf_op jit(solution)/shard_map/pallas_call | solution.py:274
  44.7 0.0 copy-start
  44.7 1.6 %copy.9 = f32[64,512]{1,0:T(8,128)} copy(f32[64,512]{1,0:T(8,128)} %get-tuple-element.4) | data formatting | bytes 262144
  46.3 0.0 copy-done
  46.3 0.7 %copy.10 = f32[64,512]{1,0:T(8,128)} copy(f32[64,512]{1,0:T(8,128)S(1)} %copy-done) | data formatting | bytes 262144
Async XLA Ops:
  44.7 1.6 %copy-start = (f32[64,512]{1,0:T(8,128)S(1)}, f32[64,512]{1,0:T(8,128)}, u32[]{:S(2)}) copy-start(f32[64,512]{1,0:T(8,128)} %get-tuple-element.5) | copy-start | bytes 393220

commit v3 on v2

--- a/solution.py
+++ b/solution.py
@@ -23,7 +23,7 @@
     row_peers, col_peers,
     depth_ref, rain_ref, conv_ref, dir_ref, outlet_ref,
     level_ref, discharge_ref,
-    depth_ext, rain_ext, coef_ext, route_ext, far_ext, acc_ext, plain,
+    depth_ext, rain_ext, coef_ext, route_ext, far_ext, acc_ext, plain, pack_out, pack_in,
     acc, rain, coef, level, share, masks,
     send_sem, recv_sem,
 ):
@@ -69,6 +69,7 @@
 
     every = (1, 3, 5, 7, 2, 6, 0, 4)
     slanted = (1, 3, 5, 7, 2, 6)
+    straight, corners = (2, 6, 0, 4), (1, 3, 5, 7)
 
     def send(slot, src, dst, width, order=every):
         for k in order:
@@ -215,11 +216,65 @@
 
     sub = lax.broadcasted_iota(jnp.int32, (SUB, LANES), 0)
 
-    def widen(src, dst, slot, meanwhile, fields):
+    lane_part = lax.broadcasted_iota(jnp.int32, (SUB, LANES), 1) // MARGIN
+
+    def corner(group, k):
+        dr, dc = OFFSETS[k]
+        slot = level_slot + group
+        return pltpu.make_async_remote_copy(
+            src_ref=pack_out.at[group, k],
+            dst_ref=pack_in.at[group, k],
+            send_sem=send_sem.at[slot, k],
+            recv_sem=recv_sem.at[slot, k],
+            device_id=(my_row + dr, my_col + dc),
+            device_id_type=MESH,
+        )
+
+    def send_corners(group, src):
+        for k in corners:
+            dr, dc = OFFSETS[k]
+            start = 0 if dr < 0 else rows - MARGIN
+            block, first = (0, 0) if dc < 0 else (own - 1, LANES - MARGIN)
+            packed = None
+            for g in range(MARGIN // SUB):
+                piece = src[block, pl.ds(start + g * SUB, SUB), :]
+                shift = (g * MARGIN - first) % LANES
+                piece = pltpu.roll(piece, shift, 1) if shift else piece
+                packed = piece if packed is None else jnp.where(lane_part == g, piece, packed)
+            pack_out[group, k] = packed
+        for k in corners:
+            @pl.when(exists(*OFFSETS[k]))
+            def _(k=k):
+                corner(group, k).start()
+
+    def receive_corners(group, dst):
+        for k in corners:
+            dr, dc = OFFSETS[k]
+            there = exists(-dr, -dc)
+            start = rows if dr < 0 else total - MARGIN
+            block, first = (own, 0) if dc < 0 else (own + 1, LANES - MARGIN)
+
+            @pl.when(there)
+            def _(k=k, start=start, block=block, first=first):
+                corner(group, k).wait_recv()
+                packed = pack_in[group, k]
+                for g in range(MARGIN // SUB):
+                    shift = (first - g * MARGIN) % LANES
+                    piece = pltpu.roll(packed, shift, 1) if shift else packed
+                    dst[block, pl.ds(start + g * SUB, SUB), :] = piece
+
+            @pl.when(jnp.logical_not(there))
+            def _(start=start, block=block):
+                dst[block, pl.ds(start, MARGIN), :] = jnp.zeros((MARGIN, LANES), dst.dtype)
+
+    def widen(src, dst, group, meanwhile, fields):
+        slot = level_slot + group
         to_plain(acc, src)
-        send(slot, src, dst, MARGIN)
+        send_corners(group, src)
+        send(slot, src, dst, MARGIN, straight)
         meanwhile()
-        receive(slot, src, dst, MARGIN)
+        receive(slot, src, dst, MARGIN, straight)
+        receive_corners(group, dst)
         for v in range(bands):
             inner = sub * bands + v < rows
             for c in range(own):
@@ -241,10 +296,10 @@
         receive(far_slot, far_ext, far_ext, MARGIN, slanted)
         set_masks(far_ext)
 
-    widen(plain.at[0], acc_ext.at[0], level_slot, in_flight, (acc, level))
+    widen(plain.at[0], acc_ext.at[0], 0, in_flight, (acc, level))
     passes(MARGIN)
     for group in range(1, GROUPS):
-        widen(plain.at[group], acc_ext.at[group], level_slot + group, lambda: None, (acc,))
+        widen(plain.at[group], acc_ext.at[group], group, lambda: None, (acc,))
         passes(MARGIN)
 
     to_plain(acc, plain.at[GROUPS])
@@ -254,7 +309,11 @@
         sent_out(slot, ext, ext, NEAR)
     sent_out(far_slot, far_ext, far_ext, MARGIN, slanted)
     for group in range(GROUPS):
-        sent_out(level_slot + group, plain.at[group], acc_ext.at[group], MARGIN)
+        sent_out(level_slot + group, plain.at[group], acc_ext.at[group], MARGIN, straight)
+        for k in corners:
+            @pl.when(exists(*OFFSETS[k]))
+            def _(group=group, k=k):
+                corner(group, k).wait_send()
 
 
 def solution(mesh):
@@ -284,6 +343,8 @@
                 pltpu.VMEM(ext, jnp.int32),
                 pltpu.VMEM((GROUPS,) + ext, f32),
                 pltpu.VMEM((GROUPS + 1, own, total, LANES), f32),
+                pltpu.VMEM((GROUPS, len(OFFSETS), SUB, LANES), f32),
+                pltpu.VMEM((GROUPS, len(OFFSETS), SUB, LANES), f32),
                 pltpu.VMEM(field, f32),
                 pltpu.VMEM(field, f32),
                 pltpu.VMEM(field, f32),

time: 47.1 us -> 45.9 us (0.975)
  Pallas kernels: 44 us -> 42.9 us
    pallas_call x1, Pallas kernels: 44 us -> 42.9 us  [on_device(): pl.pallas_call(functools.partial(kernel, row_peers, col_peers), out_shape...]
where the time goes in v3:
time: 45.9 us; the launch traced here: 45.8 us
  Pallas kernels  42.9 us (93%)
  local copies, waits for them, and re-layouts  2.26 us (5%)
  between operations  0.65 us (1%)
    pallas_call x1, Pallas kernels, on_device(): pl.pallas_call(functools.partial(kernel, row_peers, col_peers), out_shape...  42.9 us
    unnamed x4, local copies, waits for them, and re-layouts  2.26 us

profile of v3, /device:TPU:0, one launch (start us, length us, event | category | flops | bytes accessed | tf_op | source)
XLA Modules:
  0.0 45.8 jit_solution(10790626064781495231)
XLA Ops:
  0.6 42.9 %shard_map.68 = (f32[64,512]{1,0:T(8,128)}, f32[64,512]{1,0:T(8,128)}) custom-call(f32[64,512]{1,0:T(8,128)} %depth_ref.1, f32[64,512]{1,0:T(8,128)} %rain_ref.1, f32[64,512]{1,0:T(8,128)} %conv_ref.1, s32[64,512]{1,0:T(8,128)} %dir_ref.1, s32[64,512]{1,0:T(8,128)} %outlet_ref.1), custom_call_target="tpu_custom_call" | custom-call | tf_op jit(solution)/shard_map/pallas_call | solution.py:333
  43.5 0.0 copy-start
  43.5 1.6 %copy.9 = f32[64,512]{1,0:T(8,128)} copy(f32[64,512]{1,0:T(8,128)} %get-tuple-element.4) | data formatting | bytes 262144
  45.1 0.0 copy-done
  45.1 0.7 %copy.10 = f32[64,512]{1,0:T(8,128)} copy(f32[64,512]{1,0:T(8,128)S(1)} %copy-done) | data formatting | bytes 262144
Async XLA Ops:
  43.5 1.6 %copy-start = (f32[64,512]{1,0:T(8,128)S(1)}, f32[64,512]{1,0:T(8,128)}, u32[]{:S(2)}) copy-start(f32[64,512]{1,0:T(8,128)} %get-tuple-element.5) | copy-start | bytes 393220

commit v4 on v3

--- a/solution.py
+++ b/solution.py
@@ -15,7 +15,7 @@
 NEAR = 8
 MARGIN = 32
 GROUPS = PASSES // MARGIN
-SPARE = 0
+SPARE = 8
 MESH = pl.DeviceIdType.MESH
 
 

time: 45.9 us -> 46.1 us (level)
  no operation moved by 1% of the time
where the time goes in v4:
time: 46.1 us; the launch traced here: 46 us
  Pallas kernels  43.1 us (93%)
  local copies, waits for them, and re-layouts  2.26 us (5%)
  between operations  0.65 us (1%)
    pallas_call x1, Pallas kernels, on_device(): pl.pallas_call(functools.partial(kernel, row_peers, col_peers), out_shape...  43.1 us
    unnamed x4, local copies, waits for them, and re-layouts  2.26 us

profile of v4, /device:TPU:0, one launch (start us, length us, event | category | flops | bytes accessed | tf_op | source)
XLA Modules:
  0.0 46.0 jit_solution(9793389289311774476)
XLA Ops:
  0.6 43.1 %shard_map.68 = (f32[64,512]{1,0:T(8,128)}, f32[64,512]{1,0:T(8,128)}) custom-call(f32[64,512]{1,0:T(8,128)} %depth_ref.1, f32[64,512]{1,0:T(8,128)} %rain_ref.1, f32[64,512]{1,0:T(8,128)} %conv_ref.1, s32[64,512]{1,0:T(8,128)} %dir_ref.1, s32[64,512]{1,0:T(8,128)} %outlet_ref.1), custom_call_target="tpu_custom_call" | custom-call | tf_op jit(solution)/shard_map/pallas_call | solution.py:333
  43.7 0.0 copy-start
  43.7 1.6 %copy.9 = f32[64,512]{1,0:T(8,128)} copy(f32[64,512]{1,0:T(8,128)} %get-tuple-element.4) | data formatting | bytes 262144
  45.3 0.0 copy-done
  45.3 0.7 %copy.10 = f32[64,512]{1,0:T(8,128)} copy(f32[64,512]{1,0:T(8,128)S(1)} %copy-done) | data formatting | bytes 262144
Async XLA Ops:
  43.7 1.6 %copy-start = (f32[64,512]{1,0:T(8,128)S(1)}, f32[64,512]{1,0:T(8,128)}, u32[]{:S(2)}) copy-start(f32[64,512]{1,0:T(8,128)} %get-tuple-element.5) | copy-start | bytes 393220
